TPU v7x, 512 devices: a whole 4x8x8 slice. The times are simulated.
512 devices in a mesh: row: 32 (over y_lo, x, core), col: 8 (over z), dp: 2 (over y_hi).
Axes of the slice: x: 4, y: 8 (y_hi: 2, y_lo: 4; y = y_hi * 4 + y_lo), z: 8, core: 2. Of those that a mesh axis runs over, the one named last changes fastest.
Arguments:
- pixels: bfloat16 [2, 3, 1024, 1024], P('dp', None, 'row', 'col'), may hold values from -6 to 6
- cotangent: bfloat16 [2, 256, 256, 1024], P('dp', 'row', 'col'), may hold values from -6 to 6
- embed_weight: bfloat16 [48, 1024], replicated, may hold values from -0.875 to 0.875
- embed_bias: float32 [1024], replicated, may hold values from -4 to 4
- layer_norm_gain: float32 [1024], replicated, may hold values from 0.5 to 1.5
- qkv_weight: bfloat16 [1024, 2304], P('row', ('col', 'dp')), may hold values from -0.1875 to 0.1875
- out_weight: bfloat16 [768, 1024], P('row', ('col', 'dp')), may hold values from -0.21875 to 0.21875
- bias_table: float32 [12, 225], replicated, may hold values from -4 to 404
- rel_index: int32 [64, 64], replicated, may hold values from 0 to 224
- shifts: int32 [2, 2], P('dp'), may hold values from 1 to 7
Outputs:
- out_weight_grad: float32 [768, 1024], P('row', ('col', 'dp'))
- embed_weight_grad: float32 [48, 1024], replicated
- embed_bias_grad: float32 [1024], replicated
- norm_gain_grad: float32 [1024], replicated
- bias_table_grad: float32 [12, 225], replicated
Inputs may be any that keep to these rules, and one draw needn't show every extreme that they name: `rel_index`: each entry names one of the 225 columns of bias_table.
All inputs are finite; a program needn't handle non-finite values.
Results may differ from a plain program's by a relative error of at most 0.023.
Values may be sent and summed in bfloat16 or wider, within the bound.
No kernel may reach another device: no remote copies, remote signals or barrier semaphores. Data moves between devices by JAX's collectives and lax.ppermute only.
A program may use at most 64 MiB of HBM per device.

v0:
```python
import jax
import jax.numpy as jnp
from jax import lax
from jax.sharding import PartitionSpec as P

WIN = 8
PATCH = 4
norm_epsilon = 1e-05


def laid_out(blocks, dim):
    blocks = jnp.moveaxis(blocks, 0, dim)
    lengths = blocks.shape
    return blocks.reshape(*lengths[:dim], lengths[dim] * lengths[dim + 1], *lengths[dim + 2 :])


def exchange(blocks, axis):
    return lax.all_to_all(blocks, axis, split_axis=0, concat_axis=0, tiled=True)


def spread(line, axis):
    copies = jnp.broadcast_to(line[None], (lax.axis_size(axis), *line.shape))
    return exchange(copies, axis)


def gather_together(arrays, axis, dims):
    line = jnp.concatenate([a.reshape(-1) for a in arrays])
    lines, at, gathered = (spread(line, axis), 0, [])
    for a, dim in zip(arrays, dims):
        blocks = lines[:, at : at + a.size].reshape(-1, *a.shape)
        gathered.append(laid_out(blocks, dim))
        at += a.size
    return tuple(gathered)


def from_behind(value, axis, steps):
    count = lax.axis_size(axis)
    pairs = [(source, (source + steps) % count) for source in range(count)]
    return lax.ppermute(value, axis, pairs)


def in_blocks(x, dim, length):
    before, after = (x.shape[:dim], x.shape[dim + 1 :])
    return jnp.moveaxis(x.reshape(*before, length, -1, *after), dim, 0)


def summed_on_arrival(x, axis, dim):
    blocks = in_blocks(x, dim, lax.axis_size(axis))
    arrived = lax.all_to_all(blocks, axis, split_axis=0, concat_axis=0, tiled=True)
    return arrived.astype(jnp.float32).sum(axis=0)


def make_patches(pixel_block):
    images, channels, pixel_rows, pixel_cols = pixel_block.shape
    grid_rows = pixel_rows // PATCH
    grid_cols = pixel_cols // PATCH
    shaped = pixel_block.reshape(images, channels, grid_rows, PATCH, grid_cols, PATCH)
    return shaped.transpose(0, 2, 4, 1, 3, 5).reshape(
        images, grid_rows, grid_cols, channels * PATCH * PATCH
    )


def embed_cells(patches, embed_weight, embed_bias):
    return (jnp.dot(patches, embed_weight, preferred_element_type=jnp.float32) + embed_bias).astype(
        jnp.bfloat16
    )


def window_split(block):
    rows_all, cols_all, features = block.shape
    shaped = block.reshape(rows_all // WIN, WIN, cols_all // WIN, WIN, features)
    return shaped.transpose(0, 2, 1, 3, 4).reshape(-1, WIN * WIN, features)


def window_join(windows, rows_all, cols_all):
    features = windows.shape[-1]
    shaped = windows.reshape(rows_all // WIN, cols_all // WIN, WIN, WIN, features)
    return shaped.transpose(0, 2, 1, 3, 4).reshape(rows_all, cols_all, features)


def splice_after(own_block, borrowed, offsets, along_dim):
    length = own_block.shape[along_dim]

    def single(own_item, borrowed_item, offset):
        joined = jnp.concatenate([own_item, borrowed_item], along_dim - 1)
        return lax.dynamic_slice_in_dim(joined, offset, length, along_dim - 1)

    return jax.vmap(single)(own_block, borrowed, offsets)


def attend_forward(cell_windows, labels, layer_norm_gain, qkv_full, bias_full):
    window_count, cell_count, features = cell_windows.shape
    head_count = bias_full.shape[0]
    inner_width = qkv_full.shape[1] // 3
    head_size = inner_width // head_count
    score_scale = head_size ** (-0.5)
    flat_rows = cell_windows.reshape(-1, features).astype(jnp.float32)
    average = jnp.mean(flat_rows, axis=-1, keepdims=True)
    centered_input = flat_rows - average
    inverse_deviation = lax.rsqrt(
        jnp.mean(centered_input * centered_input, axis=-1, keepdims=True) + norm_epsilon
    )
    standardized_rows = centered_input * inverse_deviation
    normalized_rows = (standardized_rows * layer_norm_gain).astype(jnp.bfloat16)
    projected = jnp.dot(normalized_rows, qkv_full, preferred_element_type=jnp.float32).astype(
        jnp.bfloat16
    )
    head_shape = (window_count, cell_count, head_count, head_size)
    query_rows = projected[:, :inner_width].reshape(head_shape)
    key_vectors = projected[:, inner_width : 2 * inner_width].reshape(head_shape)
    value_rows = projected[:, 2 * inner_width :].reshape(head_shape)
    scores = (
        jnp.einsum("wmhd,wnhd->whmn", query_rows, key_vectors, preferred_element_type=jnp.float32)
        * score_scale
        + bias_full[None]
    )
    same_region = labels[:, None, :, None] == labels[:, None, None, :]
    scores = jnp.where(same_region, scores, -1e30)
    row_peak = jnp.max(scores, axis=-1, keepdims=True)
    exp_scores = jnp.exp(scores - row_peak)
    attention_weights = exp_scores / jnp.sum(exp_scores, axis=-1, keepdims=True)
    reduced_probability = attention_weights.astype(jnp.bfloat16)
    attended = jnp.einsum(
        "whmn,wnhd->wmhd", reduced_probability, value_rows, preferred_element_type=jnp.float32
    ).astype(jnp.bfloat16)
    stored_residuals = (
        standardized_rows,
        inverse_deviation,
        query_rows,
        key_vectors,
        value_rows,
        attention_weights,
        reduced_probability,
    )
    return (stored_residuals, attended.reshape(-1, inner_width))


def attend_backward(stored_residuals, d_attended, layer_norm_gain, qkv_full):
    (
        standardized_rows,
        inverse_deviation,
        query_rows,
        key_vectors,
        value_rows,
        attention_weights,
        reduced_probability,
    ) = stored_residuals
    head_shape = query_rows.shape
    score_scale = head_shape[3] ** (-0.5)
    total_row_count = standardized_rows.shape[0]
    inner_width = head_shape[2] * head_shape[3]
    d_heads = d_attended.reshape(head_shape)
    d_prob = jnp.einsum("wmhd,wnhd->whmn", d_heads, value_rows, preferred_element_type=jnp.float32)
    d_values = jnp.einsum(
        "whmn,wmhd->wnhd", reduced_probability, d_heads, preferred_element_type=jnp.float32
    ).astype(jnp.bfloat16)
    d_scores = attention_weights * (
        d_prob - jnp.sum(attention_weights * d_prob, axis=-1, keepdims=True)
    )
    table_part = jnp.sum(d_scores, axis=0)
    d_low = d_scores.astype(jnp.bfloat16)
    d_queries = (
        jnp.einsum("whmn,wnhd->wmhd", d_low, key_vectors, preferred_element_type=jnp.float32)
        * score_scale
    ).astype(jnp.bfloat16)
    d_keys = (
        jnp.einsum("whmn,wmhd->wnhd", d_low, query_rows, preferred_element_type=jnp.float32)
        * score_scale
    ).astype(jnp.bfloat16)
    d_projected = jnp.concatenate(
        [
            d_queries.reshape(total_row_count, inner_width),
            d_keys.reshape(total_row_count, inner_width),
            d_values.reshape(total_row_count, inner_width),
        ],
        axis=1,
    )
    normalized_gradient = lax.dot_general(
        d_projected, qkv_full, (((1,), (1,)), ((), ())), preferred_element_type=jnp.float32
    )
    gain_contribution = jnp.sum(normalized_gradient * standardized_rows, axis=0)
    scaled_rows = normalized_gradient * layer_norm_gain
    branch_gradient = inverse_deviation * (
        scaled_rows
        - jnp.mean(scaled_rows, axis=-1, keepdims=True)
        - standardized_rows * jnp.mean(scaled_rows * standardized_rows, axis=-1, keepdims=True)
    )
    return (branch_gradient.astype(jnp.bfloat16), gain_contribution, table_part)


def on_device(
    pixels,
    cotangent,
    embed_weight,
    embed_bias,
    layer_norm_gain,
    qkv_weight,
    out_weight,
    bias_table,
    rel_index,
    shifts,
):
    images, rows_dev, cols_dev, features = cotangent.shape
    head_count = bias_table.shape[0]
    grid_rows = rows_dev * lax.axis_size("row")
    grid_cols = cols_dev * lax.axis_size("col")
    row_shift = shifts[:, 0]
    col_shift = shifts[:, 1]
    qkv_columns, out_columns = gather_together((qkv_weight, out_weight), ("col", "dp"), (1, 1))
    rows_qkv, width_qkv = qkv_columns.shape
    out_tall = out_columns.reshape(rows_qkv, -1)
    weights = lax.all_gather(
        jnp.concatenate([qkv_columns, out_tall], axis=1), "row", axis=0, tiled=True
    )
    qkv_full = weights[:, :width_qkv]
    out_full = weights[:, width_qkv:].reshape(-1, features)
    patches = make_patches(pixels)
    below = from_behind((pixels, cotangent), "row", -1)
    moved_pixels = splice_after(pixels, below[0], row_shift * PATCH, 2)
    shifted_cot = splice_after(cotangent, below[1], row_shift, 1)
    beside = from_behind((moved_pixels[:, :, :, : WIN * PATCH], shifted_cot[:, :, :WIN]), "col", -1)
    moved_pixels = splice_after(moved_pixels, beside[0], col_shift * PATCH, 3)
    shifted_cot = splice_after(shifted_cot, beside[1], col_shift, 2)
    moved_patches = make_patches(moved_pixels)
    shifted = embed_cells(moved_patches, embed_weight, embed_bias)
    row_ids = lax.axis_index("row") * rows_dev + jnp.arange(rows_dev, dtype=jnp.int32)
    col_ids = lax.axis_index("col") * cols_dev + jnp.arange(cols_dev, dtype=jnp.int32)
    row_part = (row_ids[None, :] >= grid_rows - row_shift[:, None]).astype(jnp.int32)
    col_part = (col_ids[None, :] >= grid_cols - col_shift[:, None]).astype(jnp.int32)
    region = 2 * row_part[:, :, None] + col_part[:, None, :]
    labels = window_split(region.reshape(images * rows_dev, cols_dev, 1))[:, :, 0]
    cell_windows = window_split(shifted.reshape(images * rows_dev, cols_dev, features))
    cot_flat = window_split(shifted_cot.reshape(images * rows_dev, cols_dev, features)).reshape(
        -1, features
    )
    selector = (
        rel_index.reshape(-1)[:, None] == jnp.arange(bias_table.shape[1], dtype=jnp.int32)[None, :]
    ).astype(jnp.float32)
    bias_full = jnp.dot(selector, bias_table.T, precision=lax.Precision.HIGHEST).T.reshape(
        head_count, WIN * WIN, WIN * WIN
    )
    stored_residuals, attended = attend_forward(
        cell_windows, labels, layer_norm_gain, qkv_full, bias_full
    )
    d_attended = lax.dot_general(
        cot_flat, out_full, (((1,), (1,)), ((), ())), preferred_element_type=jnp.float32
    ).astype(jnp.bfloat16)
    partial_rows = summed_on_arrival(
        lax.dot_general(
            attended, cot_flat, (((0,), (0,)), ((), ())), preferred_element_type=jnp.float32
        ).astype(jnp.bfloat16),
        "row",
        0,
    )
    d_rows, gain_contribution, table_part = attend_backward(
        stored_residuals, d_attended, layer_norm_gain, qkv_full
    )
    branch_gradient = window_join(
        d_rows.reshape(-1, WIN * WIN, features), images * rows_dev, cols_dev
    ).reshape(images, rows_dev, cols_dev, features)
    patch_rows = patches.reshape(-1, patches.shape[-1])
    cot_rows = cotangent.reshape(-1, features)
    contract = (((0,), (0,)), ((), ()))
    branch_patches = moved_patches.reshape(-1, patches.shape[-1])
    back_rows = branch_gradient.reshape(-1, features)
    embed_grad = lax.dot_general(
        patch_rows, cot_rows, contract, preferred_element_type=jnp.float32
    ) + lax.dot_general(branch_patches, back_rows, contract, preferred_element_type=jnp.float32)
    bias_grad = jnp.sum(cot_rows, axis=0, dtype=jnp.float32) + jnp.sum(
        back_rows, axis=0, dtype=jnp.float32
    )
    table_grad = jnp.dot(
        table_part.reshape(head_count, -1), selector, precision=lax.Precision.HIGHEST
    )
    head_table = table_grad.reshape(-1)
    pieces = [embed_grad.reshape(-1), bias_grad, gain_contribution, head_table]
    line = jnp.concatenate(pieces)
    row_count = lax.axis_size("row")
    piece = -(-line.size // (row_count * 1024)) * 1024
    line = jnp.pad(line, (0, row_count * piece - line.size)).reshape(row_count, piece // 128, 128)
    mine = exchange(line, "row").sum(axis=0).reshape(-1)
    col_blocks = in_blocks(partial_rows, 1, lax.axis_size(("col", "dp")))
    block_shape = col_blocks.shape
    col_blocks = col_blocks.reshape(block_shape[0], -1)
    own = jnp.broadcast_to(mine[None], (block_shape[0], piece))
    both = exchange(jnp.concatenate([own, col_blocks], axis=1), ("col", "dp")).sum(axis=0)
    out_weight_grad = both[piece:].reshape(block_shape[1:])
    total = spread(both[:piece].reshape(piece // 128, 128), "row").reshape(-1)
    results, at = ([], 0)
    for a, shape in zip(pieces, (embed_grad.shape, (features,), (features,), table_grad.shape)):
        results.append(total[at : at + a.size].reshape(shape))
        at += a.size
    return (out_weight_grad, *results)


def solution(mesh):
    return jax.shard_map(
        on_device,
        mesh=mesh,
        in_specs=(
            P("dp", None, "row", "col"),
            P("dp", "row", "col", None),
            P(),
            P(),
            P(),
            P("row", ("col", "dp")),
            P("row", ("col", "dp")),
            P(),
            P(),
            P("dp", None),
        ),
        out_specs=(P("row", ("col", "dp")), P(), P(), P(), P()),
        check_vma=False,
    )
```

profile of v0, /device:TPU:1, one launch (start us, length us, event | category | flops | bytes accessed | tf_op | source)
XLA Modules:
  0.0 269.2 jit_solution(6066088477923813417)
XLA Ops:
  7.2 0.8 reshape.251
  8.0 0.8 reshape.250
  9.6 1.8 reduce.5
  11.5 28.5 %all_to_all.33 = bf16[16,2,3072]{2,1,0:T(2,128)(2,1)S(1)} all-to-all(bf16[16,2,3072]{2,1,0:T(2,128)(2,1)S(1)} %reshape.400), channel_id=1, replica_groups=mesh['row'=32,'col'=8,'dp'=2] {'col','dp'}, dimensions={0} | all-to-all | bytes 393216 | tf_op jit(solution)/shard_map/all_to_all | solution.py:18
  42.2 3.7 %collective-permute-start = (bf16[1,3,32,128]{3,2,1,0:T(8,128)(2,1)S(1)}, bf16[1,3,32,128]{3,2,1,0:T(8,128)(2,1)S(1)}, u32[]{:S(2)}, u32[]{:S(2)}) collective-permute-start(bf16[1,3,32,128]{3,2,1,0:T(8,128)(2,1)S(1)} %copy-done.12), channel_id=1, source_target_pairs={{0,496},{16,0},{32,16},{48,32},{64,48},{80,64},{96,80},{112,96},{1... | collective-permute-start | bytes 73736 | tf_op jit(solution)/shard_map/ppermute | solution.py:39
  45.9 3.3 %collective-permute-start.2 = (bf16[1,8,32,1024]{3,2,1,0:T(8,128)(2,1)S(1)}, bf16[1,8,32,1024]{3,2,1,0:T(8,128)(2,1)S(1)}, u32[]{:S(2)}, u32[]{:S(2)}) collective-permute-start(bf16[1,8,32,1024]{3,2,1,0:T(8,128)(2,1)S(1)} %copy-done.3), channel_id=1, source_target_pairs={{0,496},{16,0},{32,16},{48,32},{64,48},{80,64},{96,80},{112,96},{1... | collective-permute-start | bytes 1572872 | tf_op jit(solution)/shard_map/ppermute | solution.py:39
  49.3 1.7 reshape.246
  54.0 2.6 convolution_bitcast_fusion
  56.5 0.9 fusion.48
  58.3 1.9 collective-permute-start.1
  63.7 0.9 copy.218
  66.1 1.7 reshape.248
  69.7 2.6 collective-permute-start.3
  73.3 2.6 collective-permute-done.3
  76.2 31.0 %all-gather.2.cloned.1.call-done = bf16[1024,3072]{1,0:T(8,128)(2,1)} async-done(((bf16[32,3072]{1,0:T(8,128)(2,1)}), bf16[1024,3072]{1,0:T(8,128)(2,1)}) %all-gather.2.cloned.1.call-update) | async-done | bytes 6291472 | tf_op jit(solution)/shard_map/all_gather | solution.py:212
  107.2 3.7 %fusion.6 = bf16[256,2304]{1,0:T(8,128)(2,1)S(1)} fusion(bf16[256,1024]{1,0:T(8,128)(2,1)S(1)} %multiply_convert_fusion.3, bf16[1024,3072]{1,0:T(8,128)(2,1)} %all-gather.2.cloned.1.call-done), kind=kOutput, calls=%fused_computation.8 | convolution fusion | flops 1208549376 | bytes 6422528 | tf_op jit(solution)/shard_map/dot_general | solution.py:105
  110.9 1.0 fusion.43
  112.5 1.0 copy.224
  113.5 1.7 reshape.398
  115.2 1.6 copy.237
  116.8 2.5 reshape.396
  119.2 1.8 copy.228
  121.0 2.7 %slice.173 = bf16[1024,768]{1,0:T(8,128)(2,1)} slice(bf16[1024,3072]{1,0:T(8,128)(2,1)} %all-gather.2.cloned.1.call-done), slice={[0:1024], [2304:3072]} | slice | bytes 3145728 | tf_op jit(solution)/shard_map/slice | solution.py:216
  123.8 3.9 %reshape.257 = bf16[768,1024]{1,0:T(8,128)(2,1)} reshape(bf16[1024,768]{1,0:T(8,128)(2,1)} %slice.173) | data formatting | bytes 3145728 | tf_op jit(solution)/shard_map/reshape | solution.py:216
  127.7 2.8 %convolution_convert_fusion.3 = bf16[256,768]{1,0:T(8,128)(2,1)} fusion(bf16[256,1024]{1,0:T(8,128)(2,1)S(1)} %bitcast.133, bf16[768,1024]{1,0:T(8,128)(2,1)} %reshape.257), kind=kOutput, calls=%fused_computation.28 | convolution fusion | flops 402849792 | bytes 2490368 | tf_op jit(solution)/shard_map/dot_general | solution.py:245
  130.4 2.5 reshape.397
  132.9 2.5 copy.232
  135.9 1.7 fusion.47
  137.6 3.6 %fusion.14 = bf16[4,64,12,64]{1,3,2,0:T(8,128)(2,1)} fusion(bf16[4,64,12,64]{1,3,2,0:T(8,128)(2,1)} %copy.232, f32[4,12,64]{2,1,0:T(8,128)S(1)} %get-tuple-element.63, f32[4,12,64,64]{2,3,1,0:T(8,128)} %copy-done.1), kind=kOutput, calls=%fused_computation.24 | convolution fusion | flops 25955392 | bytes 1585152 | tf_op jit(solution)/shard_map/whmn,wmhd->wnhd/dot_general | solution.py:154
  141.2 2.5 multiply_reduce_fusion
  143.7 1.3 fusion.29
  145.0 1.5 fusion.17
  146.4 1.5 fusion.16
  149.1 1.6 copy.227
  150.7 1.3 reshape.260
  152.0 0.8 copy.231
  153.3 4.2 %multiply_reduce_fusion.2 = (f32[256]{0:T(256)S(1)}, f32[1024]{0:T(1024)S(1)}, f32[256]{0:T(256)S(1)}, f32[256,1024]{1,0:T(8,128)S(1)}) fusion(f32[1,4,8,8,1024]{4,3,2,1,0:T(8,128)S(1)} %copy.211, f32[1024]{0:T(1024)S(1)} %copy-done.15, f32[256]{0:T(256)S(1)} %div.24, f32[256]{0:T(256)S(1)} %rsqrt.12, bf16[1024,3072]{1,0:T(8,128)(2,1)} %all-gather.2.cloned.1.call-done, ...), kind=kOutput, calls=%fused_computation.47 | convolution fusion | flops 1213594112 | bytes 8007680 | tf_op jit(solution)/shard_map/dot_general | solution.py:178
  158.8 1.4 fusion.1
  160.7 0.7 select_maximum_fusion
  161.4 5.1 %all-to-all-start.1 = ((f32[32,16,128]{2,1,0:T(8,128)}), f32[32,16,128]{2,1,0:T(8,128)S(1)}, u32[]{:S(2)}, u32[]{:S(2)}) async-start(f32[32,16,128]{2,1,0:T(8,128)} %bitcast.30), calls=%async_computation.1 | async-start | bytes 524288 | tf_op jit(solution)/shard_map/all_to_all | solution.py:18
  166.5 2.5 fusion.15
  170.1 1.7 convolution_convert_fusion
  171.8 5.7 %all-to-all-done.1 = f32[32,16,128]{2,1,0:T(8,128)S(1)} async-done(((f32[32,16,128]{2,1,0:T(8,128)}), f32[32,16,128]{2,1,0:T(8,128)S(1)}, u32[]{:S(2)}, u32[]{:S(2)}) %all-to-all-start.1) | async-done | bytes 262176 | tf_op jit(solution)/shard_map/all_to_all | solution.py:18
  177.6 3.9 %all-to-all-start.2 = ((bf16[32,24,1024]{2,1,0:T(8,128)(2,1)}), bf16[32,24,1024]{2,1,0:T(8,128)(2,1)S(1)}, u32[]{:S(2)}, u32[]{:S(2)}) async-start(bf16[32,24,1024]{2,1,0:T(8,128)(2,1)} %bitcast.33), calls=%async_computation.2 | async-start | bytes 3145728 | tf_op jit(solution)/shard_map/all_to_all | solution.py:49
  181.5 36.9 %all-to-all-done.2 = bf16[32,24,1024]{2,1,0:T(8,128)(2,1)S(1)} async-done(((bf16[32,24,1024]{2,1,0:T(8,128)(2,1)}), bf16[32,24,1024]{2,1,0:T(8,128)(2,1)S(1)}, u32[]{:S(2)}, u32[]{:S(2)}) %all-to-all-start.2) | async-done | bytes 1572896 | tf_op jit(solution)/shard_map/all_to_all | solution.py:49
  219.1 21.9 %all_to_all.34 = f32[16,1,3584]{2,1,0:T(1,128)S(1)} all-to-all(f32[16,1,3584]{2,1,0:T(1,128)S(1)} %all_to_all.25), channel_id=1, replica_groups=mesh['row'=32,'col'=8,'dp'=2] {'col','dp'}, dimensions={0} | all-to-all | bytes 458752 | tf_op jit(solution)/shard_map/all_to_all | solution.py:18
  241.9 7.4 %all-to-all-start.4 = ((f32[32,16,128]{2,1,0:T(8,128)}), f32[32,16,128]{2,1,0:T(8,128)S(1)}, u32[]{:S(2)}, u32[]{:S(2)}) async-start(f32[32,16,128]{2,1,0:T(8,128)} %broadcast_in_dim.66), calls=%async_computation.4 | async-start | bytes 524288 | tf_op jit(solution)/shard_map/all_to_all | solution.py:18
  250.0 10.4 %all-to-all-done.4 = f32[32,16,128]{2,1,0:T(8,128)S(1)} async-done(((f32[32,16,128]{2,1,0:T(8,128)}), f32[32,16,128]{2,1,0:T(8,128)S(1)}, u32[]{:S(2)}, u32[]{:S(2)}) %all-to-all-start.4) | async-done | bytes 262176 | tf_op jit(solution)/shard_map/all_to_all | solution.py:18
  (125 shorter events, 18.0 us)
Async XLA Ops:
  7.2 61.2 %copy-start = (bf16[48,1024]{1,0:T(8,128)(2,1)S(1)}, bf16[48,1024]{1,0:T(8,128)(2,1)}, u32[]{:S(2)}) copy-start(bf16[48,1024]{1,0:T(8,128)(2,1)} %param.12) | copy-start | bytes 294916
  7.2 100.0 %all-gather.2.cloned.1.call-start = ((), (), s32[]{:S(2)}) async-start(), calls=%async_computation.5 | async-start | bytes 6488064 | tf_op jit(solution)/shard_map/all_gather | solution.py:212
  40.1 2.1 copy-start.12
  40.1 5.8 %copy-start.3 = (bf16[1,8,32,1024]{3,2,1,0:T(8,128)(2,1)S(1)}, bf16[1,8,32,1024]{3,2,1,0:T(8,128)(2,1)}, u32[]{:S(2)}) copy-start(bf16[1,8,32,1024]{3,2,1,0:T(8,128)(2,1)} %param.11) | copy-start | bytes 1572868
  40.4 10.6 %copy-start.19 = (s32[1,2]{1,0:T(1,128)S(1)}, s32[1,2]{1,0:T(1,128)}, u32[]{:S(2)}) copy-start(s32[1,2]{1,0:T(1,128)} %param.19) | copy-start | bytes 28
  40.4 12.7 %copy-start.14 = (s32[64,64]{1,0:T(8,128)S(1)}, s32[64,64]{1,0:T(8,128)}, u32[]{:S(2)}) copy-start(s32[64,64]{1,0:T(8,128)} %param.18) | copy-start | bytes 49156
  41.2 12.8 %copy-start.20 = (f32[12,225]{1,0:T(8,128)S(1)}, f32[12,225]{1,0:T(8,128)}, u32[]{:S(2)}) copy-start(f32[12,225]{1,0:T(8,128)} %param.17) | copy-start | bytes 32404
  42.2 16.0 %collective-permute-start = (bf16[1,3,32,128]{3,2,1,0:T(8,128)(2,1)S(1)}, bf16[1,3,32,128]{3,2,1,0:T(8,128)(2,1)S(1)}, u32[]{:S(2)}, u32[]{:S(2)}) collective-permute-start(bf16[1,3,32,128]{3,2,1,0:T(8,128)(2,1)S(1)} %copy-done.12), channel_id=1, source_target_pairs={{0,496},{16,0},{32,16},{48,32},{64,48},{80,64},{96,80},{112,96},{1... | collective-permute-start | bytes 73736 | tf_op jit(solution)/shard_map/ppermute | solution.py:39
  45.9 23.5 %collective-permute-start.2 = (bf16[1,8,32,1024]{3,2,1,0:T(8,128)(2,1)S(1)}, bf16[1,8,32,1024]{3,2,1,0:T(8,128)(2,1)S(1)}, u32[]{:S(2)}, u32[]{:S(2)}) collective-permute-start(bf16[1,8,32,1024]{3,2,1,0:T(8,128)(2,1)S(1)} %copy-done.3), channel_id=1, source_target_pairs={{0,496},{16,0},{32,16},{48,32},{64,48},{80,64},{96,80},{112,96},{1... | collective-permute-start | bytes 1572872 | tf_op jit(solution)/shard_map/ppermute | solution.py:39
  53.1 5.1 %copy-start.16 = (s32[4096]{0:T(1024)}, s32[4096]{0:T(1024)S(1)}, u32[]{:S(2)}) copy-start(s32[4096]{0:T(1024)S(1)} %eq.39) | copy-start | bytes 49156
  58.3 7.7 %collective-permute-start.1 = (bf16[1,3,32,32]{3,2,1,0:T(8,128)(2,1)S(1)}, bf16[1,3,32,32]{3,2,1,0:T(8,128)(2,1)S(1)}, u32[]{:S(2)}, u32[]{:S(2)}) collective-permute-start(bf16[1,3,32,32]{3,2,1,0:T(8,128)(2,1)S(1)} %bitcast.145), channel_id=1, source_target_pairs={{0,14},{2,0},{4,2},{6,4},{8,6},{10,8},{12,10},{14,12},{1,15},{3,1}... | collective-permute-start | bytes 18440 | tf_op jit(solution)/shard_map/ppermute | solution.py:39
  63.5 4.9 %copy-start.18 = (f32[1024]{0:T(1024)S(1)}, f32[1024]{0:T(1024)}, u32[]{:S(2)}) copy-start(f32[1024]{0:T(1024)} %param.13) | copy-start | bytes 12292
  69.1 3.2 %copy-start.15 = (f32[1024]{0:T(1024)S(1)}, f32[1024]{0:T(1024)}, u32[]{:S(2)}) copy-start(f32[1024]{0:T(1024)} %param.14) | copy-start | bytes 12292
  69.7 6.1 %collective-permute-start.3 = (bf16[1,8,8,1024]{3,2,1,0:T(8,128)(2,1)S(1)}, bf16[1,8,8,1024]{3,2,1,0:T(8,128)(2,1)S(1)}, u32[]{:S(2)}, u32[]{:S(2)}) collective-permute-start(bf16[1,8,8,1024]{3,2,1,0:T(8,128)(2,1)S(1)} %slice.172), channel_id=1, source_target_pairs={{0,14},{2,0},{4,2},{6,4},{8,6},{10,8},{12,10},{14,12},{1,15},{3,1}... | collective-permute-start | bytes 393224 | tf_op jit(solution)/shard_map/ppermute | solution.py:39
  76.2 51.5 %copy-start.5 = (bf16[1,4,8,8,1024]{4,3,2,1,0:T(8,128)(2,1)}, bf16[1,4,8,8,1024]{4,3,2,1,0:T(8,128)(2,1)S(1)}, u32[]{:S(2)}) copy-start(bf16[1,4,8,8,1024]{4,3,2,1,0:T(8,128)(2,1)S(1)} %copy.219) | copy-start | bytes 1572868
  130.4 5.0 %copy-start.7 = (f32[12,64,64]{1,2,0:T(8,128)S(1)}, f32[12,64,64]{1,2,0:T(8,128)}, u32[]{:S(2)}) copy-start(f32[12,64,64]{1,2,0:T(8,128)} %copy.218) | copy-start | bytes 589828
  135.9 1.7 copy-start.1
  141.2 2.5 copy-start.2
  146.4 1.5 copy-start.10
  149.1 2.9 %copy-start.4 = (bf16[4,64,12,64]{3,1,2,0:T(8,128)(2,1)S(1)}, bf16[4,64,12,64]{3,1,2,0:T(8,128)(2,1)}, u32[]{:S(2)}) copy-start(bf16[4,64,12,64]{3,1,2,0:T(8,128)(2,1)} %fusion.17) | copy-start | bytes 1179652
  157.5 1.0 copy-start.8
  157.9 0.9 copy-start.17
  158.0 2.3 copy-start.11
  158.0 2.3 copy-start.13
  158.8 7.7 %copy-start.9 = (bf16[4,64,12,64]{1,3,2,0:T(8,128)(2,1)S(1)}, bf16[4,64,12,64]{1,3,2,0:T(8,128)(2,1)}, u32[]{:S(2)}) copy-start(bf16[4,64,12,64]{1,3,2,0:T(8,128)(2,1)} %copy.237) | copy-start | bytes 1179652
  161.4 16.2 %all-to-all-start.1 = ((f32[32,16,128]{2,1,0:T(8,128)}), f32[32,16,128]{2,1,0:T(8,128)S(1)}, u32[]{:S(2)}, u32[]{:S(2)}) async-start(f32[32,16,128]{2,1,0:T(8,128)} %bitcast.30), calls=%async_computation.1 | async-start | bytes 524288 | tf_op jit(solution)/shard_map/all_to_all | solution.py:18
  169.0 1.1 copy-start.6
  177.6 40.9 %all-to-all-start.2 = ((bf16[32,24,1024]{2,1,0:T(8,128)(2,1)}), bf16[32,24,1024]{2,1,0:T(8,128)(2,1)S(1)}, u32[]{:S(2)}, u32[]{:S(2)}) async-start(bf16[32,24,1024]{2,1,0:T(8,128)(2,1)} %bitcast.33), calls=%async_computation.2 | async-start | bytes 3145728 | tf_op jit(solution)/shard_map/all_to_all | solution.py:49
  241.9 18.4 %all-to-all-start.4 = ((f32[32,16,128]{2,1,0:T(8,128)}), f32[32,16,128]{2,1,0:T(8,128)S(1)}, u32[]{:S(2)}, u32[]{:S(2)}) async-start(f32[32,16,128]{2,1,0:T(8,128)} %broadcast_in_dim.66), calls=%async_computation.4 | async-start | bytes 524288 | tf_op jit(solution)/shard_map/all_to_all | solution.py:18
Sparse Core Ops, SparseCore 0:
  42.3 64.7 all-gather.1
where the time goes:
time: 270 us; the launch traced here: 269 us
  waiting for transfers between devices  86.7 us (32%)
  blocking collectives  50.4 us (19%)
  local copies, waits for them, and re-layouts  44.5 us (16%)
  matrix products  30 us (11%)
  starting transfers between devices  27.9 us (10%)
  between operations  21.3 us (8%)
  other arithmetic  8.47 us (3%)
    all_to_all x2, blocking collectives, exchange(): return lax.all_to_all(blocks, axis, split_axis=0, concat_axis=0, tiled=True)  50.4 us
    all_to_all x1, waiting for transfers between devices, summed_on_arrival(): lax.all_to_all(blocks, axis, split_axis=0, concat_axis=0, tiled=True)  36.9 us
    all_gather x1, waiting for transfers between devices, on_device(): lax.all_gather(jnp.concatenate([qkv_columns, out_tall], axis=1), 'row', a...  31 us
    all_to_all x2, waiting for transfers between devices, exchange(): return lax.all_to_all(blocks, axis, split_axis=0, concat_axis=0, tiled=True)  16.1 us
    all_to_all x2, starting transfers between devices, exchange(): return lax.all_to_all(blocks, axis, split_axis=0, concat_axis=0, tiled=True)  12.5 us
    ppermute x4, starting transfers between devices, from_behind(): return lax.ppermute(value, axis, pairs)  11.6 us
  transfers between devices with their start and end apart: 8, of which 5 were waited for; matrix products, arithmetic and copies ran while one was open for 7% of the time, Pallas kernels for 0%

commit v1 on v0

--- a/solution.py
+++ b/solution.py
@@ -209,8 +209,14 @@
     qkv_columns, out_columns = gather_together((qkv_weight, out_weight), ("col", "dp"), (1, 1))
     rows_qkv, width_qkv = qkv_columns.shape
     out_tall = out_columns.reshape(rows_qkv, -1)
-    weights = lax.all_gather(
-        jnp.concatenate([qkv_columns, out_tall], axis=1), "row", axis=0, tiled=True
+    weights = jnp.concatenate(
+        lax.all_to_all(
+            jnp.stack([jnp.concatenate([qkv_columns, out_tall], axis=1)] * lax.axis_size("row")),
+            "row",
+            0,
+            0,
+        ),
+        axis=0,
     )
     qkv_full = weights[:, :width_qkv]
     out_full = weights[:, width_qkv:].reshape(-1, features)

time: 270 us -> 353 us (1.31)
  waiting for transfers between devices: 86.7 us -> 157 us
  starting transfers between devices: 27.9 us -> 56.2 us
  between operations: 21.3 us -> 7.9 us
  blocking collectives: 50.4 us -> 46.2 us
    all_to_all x0 -> x1, waiting for transfers between devices: none -> 77.6 us  [on_device(): lax.all_to_all(jnp.stack([jnp.concatenate([qkv_columns, out_tall], axis=1...]
    all_gather x1 -> x0, waiting for transfers between devices: 31 us -> none  [on_device(): lax.all_gather(jnp.concatenate([qkv_columns, out_tall], axis=1), 'row', a...]
    ppermute x4, waiting for transfers between devices: 2.56 us -> 26.8 us  [from_behind(): return lax.ppermute(value, axis, pairs)]
    all_to_all x2, starting transfers between devices: 12.5 us -> 30 us  [exchange(): return lax.all_to_all(blocks, axis, split_axis=0, concat_axis=0, tiled=True)]
    all_to_all x0 -> x1, starting transfers between devices: none -> 8.38 us  [on_device(): lax.all_to_all(jnp.stack([jnp.concatenate([qkv_columns, out_tall], axis=1...]
    all_to_all x2, blocking collectives: 50.4 us -> 46.2 us  [exchange(): return lax.all_to_all(blocks, axis, split_axis=0, concat_axis=0, tiled=True)]
  transfers between devices with their start and end apart: 8 -> 8, of which waited for: 5 -> 7; matrix products, arithmetic and copies ran while one was open for 7% -> 6% of each run, Pallas kernels for 0% -> 0%
where the time goes in v1:
time: 353 us; the launch traced here: 352 us
  waiting for transfers between devices  157 us (44%)
  starting transfers between devices  56.2 us (16%)
  local copies, waits for them, and re-layouts  47.6 us (13%)
  blocking collectives  46.2 us (13%)
  matrix products  27.8 us (8%)
  other arithmetic  8.6 us (2%)
  between operations  7.9 us (2%)
    all_to_all x1, waiting for transfers between devices, on_device(): lax.all_to_all(jnp.stack([jnp.concatenate([qkv_columns, out_tall], axis=1...  77.6 us
    all_to_all x2, blocking collectives, exchange(): return lax.all_to_all(blocks, axis, split_axis=0, concat_axis=0, tiled=True)  46.2 us
    all_to_all x1, waiting for transfers between devices, summed_on_arrival(): lax.all_to_all(blocks, axis, split_axis=0, concat_axis=0, tiled=True)  36.9 us
    all_to_all x2, starting transfers between devices, exchange(): return lax.all_to_all(blocks, axis, split_axis=0, concat_axis=0, tiled=True)  30 us
    ppermute x4, waiting for transfers between devices, from_behind(): return lax.ppermute(value, axis, pairs)  26.8 us
    all_to_all x2, waiting for transfers between devices, exchange(): return lax.all_to_all(blocks, axis, split_axis=0, concat_axis=0, tiled=True)  16.1 us
    ppermute x4, starting transfers between devices, from_behind(): return lax.ppermute(value, axis, pairs)  13.9 us
    all_to_all x1, starting transfers between devices, on_device(): lax.all_to_all(jnp.stack([jnp.concatenate([qkv_columns, out_tall], axis=1...  8.38 us
  transfers between devices with their start and end apart: 8, of which 7 were waited for; matrix products, arithmetic and copies ran while one was open for 6% of the time, Pallas kernels for 0%

profile of v1, /device:TPU:1, one launch (start us, length us, event | category | flops | bytes accessed | tf_op | source)
XLA Modules:
  0.0 351.6 jit_solution(8650030437537371208)
XLA Ops:
  1.5 0.8 reshape.255
  3.0 1.8 reduce.5
  4.9 28.5 %all_to_all.38 = bf16[16,2,3072]{2,1,0:T(2,128)(2,1)S(1)} all-to-all(bf16[16,2,3072]{2,1,0:T(2,128)(2,1)S(1)} %reshape.406), channel_id=1, replica_groups=mesh['row'=32,'col'=8,'dp'=2] {'col','dp'}, dimensions={0} | all-to-all | bytes 393216 | tf_op jit(solution)/shard_map/all_to_all | solution.py:18
  34.9 3.4 stack.2
  38.4 8.4 %all-to-all-start.1 = ((bf16[32,32,3072]{2,1,0:T(8,128)(2,1)}), bf16[32,32,3072]{2,1,0:T(8,128)(2,1)}, u32[]{:S(2)}, u32[]{:S(2)}) async-start(bf16[32,32,3072]{2,1,0:T(8,128)(2,1)} %stack.2), calls=%async_computation.1 | async-start | bytes 12582912 | tf_op jit(solution)/shard_map/all_to_all | solution.py:213
  46.8 2.2 collective-permute-start
  49.0 7.4 %collective-permute-start.2 = (bf16[1,8,32,1024]{3,2,1,0:T(8,128)(2,1)S(1)}, bf16[1,8,32,1024]{3,2,1,0:T(8,128)(2,1)S(1)}, u32[]{:S(2)}, u32[]{:S(2)}) collective-permute-start(bf16[1,8,32,1024]{3,2,1,0:T(8,128)(2,1)S(1)} %copy-done.3), channel_id=1, source_target_pairs={{0,496},{16,0},{32,16},{48,32},{64,48},{80,64},{96,80},{112,96},{1... | collective-permute-start | bytes 1572872 | tf_op jit(solution)/shard_map/ppermute | solution.py:39
  56.4 1.7 reshape.251
  61.0 2.6 convolution_bitcast_fusion
  63.6 0.9 fusion.48
  65.3 20.8 %collective-permute-done = bf16[1,3,32,128]{3,2,1,0:T(8,128)(2,1)S(1)} collective-permute-done((bf16[1,3,32,128]{3,2,1,0:T(8,128)(2,1)S(1)}, bf16[1,3,32,128]{3,2,1,0:T(8,128)(2,1)S(1)}, u32[]{:S(2)}, u32[]{:S(2)}) %collective-permute-start) | collective-permute-done | bytes 24608 | tf_op jit(solution)/shard_map/ppermute | solution.py:39
  86.1 2.2 collective-permute-start.1
  91.8 0.9 copy.218
  94.1 1.7 reshape.253
  97.5 3.9 %collective-permute-done.2 = bf16[1,8,32,1024]{3,2,1,0:T(8,128)(2,1)S(1)} collective-permute-done((bf16[1,8,32,1024]{3,2,1,0:T(8,128)(2,1)S(1)}, bf16[1,8,32,1024]{3,2,1,0:T(8,128)(2,1)S(1)}, u32[]{:S(2)}, u32[]{:S(2)}) %collective-permute-start.2) | collective-permute-done | bytes 524320 | tf_op jit(solution)/shard_map/ppermute | solution.py:39
  101.6 2.2 collective-permute-start.3
  103.8 1.1 multiply_convert_fusion.3
  105.6 2.1 collective-permute-done.3
  108.1 77.6 %all-to-all-done.1 = bf16[32,32,3072]{2,1,0:T(8,128)(2,1)} async-done(((bf16[32,32,3072]{2,1,0:T(8,128)(2,1)}), bf16[32,32,3072]{2,1,0:T(8,128)(2,1)}, u32[]{:S(2)}, u32[]{:S(2)}) %all-to-all-start.1) | async-done | bytes 6291488 | tf_op jit(solution)/shard_map/all_to_all | solution.py:213
  185.6 2.7 slice.173
  188.4 3.7 %fusion.6 = bf16[256,2304]{1,0:T(8,128)(2,1)S(1)} fusion(bf16[256,1024]{1,0:T(8,128)(2,1)S(1)} %copy-done.12, bf16[1024,3072]{1,0:T(8,128)(2,1)} %bitcast.15), kind=kOutput, calls=%fused_computation.8 | convolution fusion | flops 1208549376 | bytes 6422528 | tf_op jit(solution)/shard_map/dot_general | solution.py:105
  192.1 1.0 fusion.43
  193.7 1.0 copy.224
  194.7 1.7 reshape.404
  196.4 1.6 copy.237
  198.0 2.5 reshape.402
  200.5 1.8 copy.228
  202.3 4.0 %reshape.263 = bf16[768,1024]{1,0:T(8,128)(2,1)} reshape(bf16[1024,768]{1,0:T(8,128)(2,1)} %slice.173) | data formatting | bytes 3145728 | tf_op jit(solution)/shard_map/reshape | solution.py:222
  206.3 2.8 convolution_convert_fusion.3
  209.0 2.5 reshape.403
  211.5 2.5 copy.232
  214.5 1.7 fusion.47
  216.2 3.7 %fusion.14 = bf16[4,64,12,64]{1,3,2,0:T(8,128)(2,1)} fusion(bf16[4,64,12,64]{1,3,2,0:T(8,128)(2,1)} %copy.232, f32[4,12,64]{2,1,0:T(8,128)S(1)} %get-tuple-element.63, f32[4,12,64,64]{2,3,1,0:T(8,128)} %copy-done.1), kind=kOutput, calls=%fused_computation.24 | convolution fusion | flops 25955392 | bytes 1585152 | tf_op jit(solution)/shard_map/whmn,wmhd->wnhd/dot_general | solution.py:154
  219.9 2.3 multiply_reduce_fusion
  222.2 1.2 fusion.29
  225.7 1.2 reshape.268
  228.0 0.8 copy.231
  229.3 4.1 %multiply_reduce_fusion.2 = (f32[256]{0:T(256)S(1)}, f32[1024]{0:T(1024)S(1)}, f32[256]{0:T(256)S(1)}, f32[256,1024]{1,0:T(8,128)S(1)}) fusion(f32[1,4,8,8,1024]{4,3,2,1,0:T(8,128)S(1)} %copy.211, f32[1024]{0:T(1024)S(1)} %copy-done.17, f32[256]{0:T(256)S(1)} %div.24, f32[256]{0:T(256)S(1)} %rsqrt.12, bf16[1024,3072]{1,0:T(8,128)(2,1)} %bitcast.15, ...), kind=kOutput, calls=%fused_computation.47 | convolution fusion | flops 1213594112 | bytes 8007680 | tf_op jit(solution)/shard_map/dot_general | solution.py:178
  234.7 1.4 fusion.1
  237.3 22.6 %all-to-all-start.2 = ((f32[32,16,128]{2,1,0:T(8,128)}), f32[32,16,128]{2,1,0:T(8,128)S(1)}, u32[]{:S(2)}, u32[]{:S(2)}) async-start(f32[32,16,128]{2,1,0:T(8,128)} %bitcast.31), calls=%async_computation.2 | async-start | bytes 524288 | tf_op jit(solution)/shard_map/all_to_all | solution.py:18
  259.9 2.5 fusion.15
  263.5 1.7 convolution_convert_fusion
  265.2 5.7 %all-to-all-done.2 = f32[32,16,128]{2,1,0:T(8,128)S(1)} async-done(((f32[32,16,128]{2,1,0:T(8,128)}), f32[32,16,128]{2,1,0:T(8,128)S(1)}, u32[]{:S(2)}, u32[]{:S(2)}) %all-to-all-start.2) | async-done | bytes 262176 | tf_op jit(solution)/shard_map/all_to_all | solution.py:18
  271.0 3.9 %all-to-all-start.3 = ((bf16[32,24,1024]{2,1,0:T(8,128)(2,1)}), bf16[32,24,1024]{2,1,0:T(8,128)(2,1)S(1)}, u32[]{:S(2)}, u32[]{:S(2)}) async-start(bf16[32,24,1024]{2,1,0:T(8,128)(2,1)} %bitcast.34), calls=%async_computation.3 | async-start | bytes 3145728 | tf_op jit(solution)/shard_map/all_to_all | solution.py:49
  274.9 36.9 %all-to-all-done.3 = bf16[32,24,1024]{2,1,0:T(8,128)(2,1)S(1)} async-done(((bf16[32,24,1024]{2,1,0:T(8,128)(2,1)}), bf16[32,24,1024]{2,1,0:T(8,128)(2,1)S(1)}, u32[]{:S(2)}, u32[]{:S(2)}) %all-to-all-start.3) | async-done | bytes 1572896 | tf_op jit(solution)/shard_map/all_to_all | solution.py:49
  312.5 17.7 %all_to_all.39 = f32[16,1,3584]{2,1,0:T(1,128)S(1)} all-to-all(f32[16,1,3584]{2,1,0:T(1,128)S(1)} %all_to_all.29), channel_id=1, replica_groups=mesh['row'=32,'col'=8,'dp'=2] {'col','dp'}, dimensions={0} | all-to-all | bytes 458752 | tf_op jit(solution)/shard_map/all_to_all | solution.py:18
  331.1 7.4 %all-to-all-start.5 = ((f32[32,16,128]{2,1,0:T(8,128)}), f32[32,16,128]{2,1,0:T(8,128)S(1)}, u32[]{:S(2)}, u32[]{:S(2)}) async-start(f32[32,16,128]{2,1,0:T(8,128)} %broadcast_in_dim.66), calls=%async_computation.5 | async-start | bytes 524288 | tf_op jit(solution)/shard_map/all_to_all | solution.py:18
  339.1 10.4 %all-to-all-done.5 = f32[32,16,128]{2,1,0:T(8,128)S(1)} async-done(((f32[32,16,128]{2,1,0:T(8,128)}), f32[32,16,128]{2,1,0:T(8,128)S(1)}, u32[]{:S(2)}, u32[]{:S(2)}) %all-to-all-start.5) | async-done | bytes 262176 | tf_op jit(solution)/shard_map/all_to_all | solution.py:18
  (129 shorter events, 20.8 us)
Async XLA Ops:
  0.6 95.9 %copy-start = (bf16[48,1024]{1,0:T(8,128)(2,1)S(1)}, bf16[48,1024]{1,0:T(8,128)(2,1)}, u32[]{:S(2)}) copy-start(bf16[48,1024]{1,0:T(8,128)(2,1)} %param.12) | copy-start | bytes 294916
  38.4 8.4 %copy-start.14 = (bf16[1,3,32,128]{3,2,1,0:T(8,128)(2,1)S(1)}, bf16[1,3,32,128]{3,2,1,0:T(8,128)(2,1)}, u32[]{:S(2)}) copy-start(bf16[1,3,32,128]{3,2,1,0:T(8,128)(2,1)} %param.10) | copy-start | bytes 73732
  38.4 10.6 %copy-start.3 = (bf16[1,8,32,1024]{3,2,1,0:T(8,128)(2,1)S(1)}, bf16[1,8,32,1024]{3,2,1,0:T(8,128)(2,1)}, u32[]{:S(2)}) copy-start(bf16[1,8,32,1024]{3,2,1,0:T(8,128)(2,1)} %param.11) | copy-start | bytes 1572868
  38.4 19.7 %copy-start.21 = (s32[1,2]{1,0:T(1,128)S(1)}, s32[1,2]{1,0:T(1,128)}, u32[]{:S(2)}) copy-start(s32[1,2]{1,0:T(1,128)} %param.19) | copy-start | bytes 28
  38.4 21.8 %copy-start.16 = (s32[64,64]{1,0:T(8,128)S(1)}, s32[64,64]{1,0:T(8,128)}, u32[]{:S(2)}) copy-start(s32[64,64]{1,0:T(8,128)} %param.18) | copy-start | bytes 49156
  38.4 147.3 %all-to-all-start.1 = ((bf16[32,32,3072]{2,1,0:T(8,128)(2,1)}), bf16[32,32,3072]{2,1,0:T(8,128)(2,1)}, u32[]{:S(2)}, u32[]{:S(2)}) async-start(bf16[32,32,3072]{2,1,0:T(8,128)(2,1)} %stack.2), calls=%async_computation.1 | async-start | bytes 12582912 | tf_op jit(solution)/shard_map/all_to_all | solution.py:213
  46.8 14.3 %copy-start.22 = (f32[12,225]{1,0:T(8,128)S(1)}, f32[12,225]{1,0:T(8,128)}, u32[]{:S(2)}) copy-start(f32[12,225]{1,0:T(8,128)} %param.17) | copy-start | bytes 32404
  46.8 39.2 %collective-permute-start = (bf16[1,3,32,128]{3,2,1,0:T(8,128)(2,1)S(1)}, bf16[1,3,32,128]{3,2,1,0:T(8,128)(2,1)S(1)}, u32[]{:S(2)}, u32[]{:S(2)}) collective-permute-start(bf16[1,3,32,128]{3,2,1,0:T(8,128)(2,1)S(1)} %copy-done.14), channel_id=1, source_target_pairs={{0,496},{16,0},{32,16},{48,32},{64,48},{80,64},{96,80},{112,96},{1... | collective-permute-start | bytes 73736 | tf_op jit(solution)/shard_map/ppermute | solution.py:39
  49.0 52.4 %collective-permute-start.2 = (bf16[1,8,32,1024]{3,2,1,0:T(8,128)(2,1)S(1)}, bf16[1,8,32,1024]{3,2,1,0:T(8,128)(2,1)S(1)}, u32[]{:S(2)}, u32[]{:S(2)}) collective-permute-start(bf16[1,8,32,1024]{3,2,1,0:T(8,128)(2,1)S(1)} %copy-done.3), channel_id=1, source_target_pairs={{0,496},{16,0},{32,16},{48,32},{64,48},{80,64},{96,80},{112,96},{1... | collective-permute-start | bytes 1572872 | tf_op jit(solution)/shard_map/ppermute | solution.py:39
  60.2 28.2 %copy-start.18 = (s32[4096]{0:T(1024)}, s32[4096]{0:T(1024)S(1)}, u32[]{:S(2)}) copy-start(s32[4096]{0:T(1024)S(1)} %eq.39) | copy-start | bytes 49156
  86.1 7.9 %collective-permute-start.1 = (bf16[1,3,32,32]{3,2,1,0:T(8,128)(2,1)S(1)}, bf16[1,3,32,32]{3,2,1,0:T(8,128)(2,1)S(1)}, u32[]{:S(2)}, u32[]{:S(2)}) collective-permute-start(bf16[1,3,32,32]{3,2,1,0:T(8,128)(2,1)S(1)} %bitcast.146), channel_id=1, source_target_pairs={{0,14},{2,0},{4,2},{6,4},{8,6},{10,8},{12,10},{14,12},{1,15},{3,1}... | collective-permute-start | bytes 18440 | tf_op jit(solution)/shard_map/ppermute | solution.py:39
  91.6 4.9 %copy-start.20 = (f32[1024]{0:T(1024)S(1)}, f32[1024]{0:T(1024)}, u32[]{:S(2)}) copy-start(f32[1024]{0:T(1024)} %param.13) | copy-start | bytes 12292
  97.1 6.7 %copy-start.17 = (f32[1024]{0:T(1024)S(1)}, f32[1024]{0:T(1024)}, u32[]{:S(2)}) copy-start(f32[1024]{0:T(1024)} %param.14) | copy-start | bytes 12292
  101.6 6.1 %collective-permute-start.3 = (bf16[1,8,8,1024]{3,2,1,0:T(8,128)(2,1)S(1)}, bf16[1,8,8,1024]{3,2,1,0:T(8,128)(2,1)S(1)}, u32[]{:S(2)}, u32[]{:S(2)}) collective-permute-start(bf16[1,8,8,1024]{3,2,1,0:T(8,128)(2,1)S(1)} %slice.172), channel_id=1, source_target_pairs={{0,14},{2,0},{4,2},{6,4},{8,6},{10,8},{12,10},{14,12},{1,15},{3,1}... | collective-permute-start | bytes 393224 | tf_op jit(solution)/shard_map/ppermute | solution.py:39
  108.1 98.2 %copy-start.4 = (bf16[1,4,8,8,1024]{4,3,2,1,0:T(8,128)(2,1)}, bf16[1,4,8,8,1024]{4,3,2,1,0:T(8,128)(2,1)S(1)}, u32[]{:S(2)}) copy-start(bf16[1,4,8,8,1024]{4,3,2,1,0:T(8,128)(2,1)S(1)} %copy.219) | copy-start | bytes 1572868
  185.6 2.7 copy-start.12
  209.0 5.0 %copy-start.6 = (f32[12,64,64]{1,2,0:T(8,128)S(1)}, f32[12,64,64]{1,2,0:T(8,128)}, u32[]{:S(2)}) copy-start(f32[12,64,64]{1,2,0:T(8,128)} %copy.218) | copy-start | bytes 589828
  214.5 1.7 copy-start.1
  216.2 3.7 %copy-start.8 = (bf16[4,64,12,64]{1,3,2,0:T(8,128)(2,1)S(1)}, bf16[4,64,12,64]{1,3,2,0:T(8,128)(2,1)}, u32[]{:S(2)}) copy-start(bf16[4,64,12,64]{1,3,2,0:T(8,128)(2,1)} %copy.237) | copy-start | bytes 1179652
  219.9 2.3 copy-start.2
  223.9 1.1 copy-start.10
  228.0 1.3 copy-start.13
  233.4 1.0 copy-start.7
  233.7 0.9 copy-start.19
  233.9 2.4 copy-start.11
  233.9 2.3 copy-start.15
  234.7 25.2 %copy-start.9 = (bf16[4,64,12,64]{1,3,2,0:T(8,128)(2,1)S(1)}, bf16[4,64,12,64]{1,3,2,0:T(8,128)(2,1)}, u32[]{:S(2)}) copy-start(bf16[4,64,12,64]{1,3,2,0:T(8,128)(2,1)} %copy.237) | copy-start | bytes 1179652
  237.3 33.7 %all-to-all-start.2 = ((f32[32,16,128]{2,1,0:T(8,128)}), f32[32,16,128]{2,1,0:T(8,128)S(1)}, u32[]{:S(2)}, u32[]{:S(2)}) async-start(f32[32,16,128]{2,1,0:T(8,128)} %bitcast.31), calls=%async_computation.2 | async-start | bytes 524288 | tf_op jit(solution)/shard_map/all_to_all | solution.py:18
  262.4 1.1 copy-start.5
  271.0 40.9 %all-to-all-start.3 = ((bf16[32,24,1024]{2,1,0:T(8,128)(2,1)}), bf16[32,24,1024]{2,1,0:T(8,128)(2,1)S(1)}, u32[]{:S(2)}, u32[]{:S(2)}) async-start(bf16[32,24,1024]{2,1,0:T(8,128)(2,1)} %bitcast.34), calls=%async_computation.3 | async-start | bytes 3145728 | tf_op jit(solution)/shard_map/all_to_all | solution.py:49
  331.1 18.4 %all-to-all-start.5 = ((f32[32,16,128]{2,1,0:T(8,128)}), f32[32,16,128]{2,1,0:T(8,128)S(1)}, u32[]{:S(2)}, u32[]{:S(2)}) async-start(f32[32,16,128]{2,1,0:T(8,128)} %broadcast_in_dim.66), calls=%async_computation.5 | async-start | bytes 524288 | tf_op jit(solution)/shard_map/all_to_all | solution.py:18
